TPU v7x, 256 devices: a whole 4x4x8 slice. The times are simulated.
256 devices in a mesh: blk: 8 (over x_hi, y), tok: 32 (over x_lo, z, core).
Axes of the slice: x: 4 (x_hi: 2, x_lo: 2; x = x_hi * 2 + x_lo), y: 4, z: 8, core: 2. Of those that a mesh axis runs over, the one named last changes fastest.
Arguments:
- states: bfloat16 [1024, 3584], P('tok'), may hold values from -30 to 30
- head: bfloat16 [3584, 262144], P(None, ('blk', 'tok')), may hold values from -0.2 to 0.2
- targets: int32 [1024], P('tok'), may hold values from 0 to 262143
- ref_loss: float32 [1024], P('tok'), may hold values from 0 to 8
- seq_ids: int32 [1024], P('tok'), may hold values from 0 to 511, never falling along the last dimension, each value on 1 to 4 neighbouring positions
Outputs:
- excess: float32 [1024], P('tok')
- seq_score: float32 [512], replicated
Inputs may be any that keep to these rules, and one draw needn't show every extreme that they name: `seq_ids`: sequence numbers never fall along the tokens; every number from 0 to 511 occurs, on 1 to 4 consecutive tokens.
All inputs are finite; a program needn't handle non-finite values.
Results may differ from a plain program's by a relative error of at most 0.0003.
Values may be sent and summed in bfloat16 or wider, within the bound.
No kernel may reach another device: no remote copies, remote signals or barrier semaphores. Data moves between devices by JAX's collectives and lax.ppermute only.
A program may use at most 64 MiB of HBM per device.

v0:
```python
import jax
import jax.numpy as jnp
from jax import lax
from jax.sharding import Mesh
from jax.sharding import PartitionSpec as P

TOK = ("tok_0", "tok_1", "tok_2")
BLK = ("blk_0", "blk_1")
BLK_TOK = ("blk_0", "blk_1", "tok_0", "tok_1", "tok_2")
very_low = -1e30


def all_in_one(value, axis):
    leaves = jax.tree.leaves(value)
    turns = sorted(range(len(leaves)), key=lambda k: -leaves[k].size)
    width = (1, *leaves[turns[0]].shape)[-1]
    lines = [
        jnp.pad(leaves[k].reshape(-1), (0, -leaves[k].size % width)).reshape(-1, width)
        for k in turns
    ]
    both, at, found = (lax.all_gather(jnp.concatenate(lines), axis), 0, {})
    for k, line in zip(turns, lines):
        section = both[:, at : at + len(line)].reshape(len(both), -1)
        found[k] = section[:, : leaves[k].size].reshape(-1, *leaves[k].shape)
        at += len(line)
    numbers = iter(range(len(leaves)))
    return jax.tree.map(lambda _: found[next(numbers)], value)


def merged_by_axis(value, axes, combine):
    for axis in axes:
        pieces = all_in_one(value, axis)
        value = jax.tree.map(lambda part: part[0], pieces)
        for k in range(1, lax.axis_size(axis)):
            value = combine(value, jax.tree.map(lambda part: part[k], pieces))
    return value


def copy_for_each(value, axis):
    devices = lax.axis_size(axis)
    return lax.all_to_all(
        jnp.broadcast_to(value[None], (devices, *value.shape)), axis, 0, 0, tiled=True
    )


def of_everyone(value, axis):
    return copy_for_each(value, axis).sum(axis=0)


def packed_total(arrays, axis):
    vector, at, gathered = (jnp.concatenate([a.reshape(-1) for a in arrays]), 0, [])
    so_far = of_everyone(vector, axis)
    for a in arrays:
        gathered.append(so_far[at : at + a.size].reshape(a.shape))
        at += a.size
    return tuple(gathered)


def absorb(highest, scaled, picked, token_rows, target_ids, head, first_col):
    logits = jnp.dot(token_rows, head, preferred_element_type=jnp.float32)
    new_high = jnp.maximum(highest, jnp.max(logits, axis=1))
    scaled = jnp.sum(jnp.exp(logits - new_high[:, None]), axis=1)
    columns = first_col + lax.iota(jnp.int32, head.shape[1])
    hits = columns[None, :] == target_ids[:, None]
    picked = jnp.sum(jnp.where(hits, logits, 0.0), axis=1)
    return (new_high, scaled, picked)


def combine_stats(left, right):
    left_high, left_scaled, left_picked = left
    right_high, right_scaled, right_picked = right
    highest = jnp.maximum(left_high, right_high)
    scaled = left_scaled * jnp.exp(left_high - highest) + right_scaled * jnp.exp(
        right_high - highest
    )
    return (highest, scaled, left_picked + right_picked)


def on_device(states, head, targets, ref_loss, seq_ids):
    cycle_size = lax.axis_size(TOK)
    first_col = (lax.axis_index(BLK) * cycle_size + lax.axis_index(TOK)) * head.shape[1]
    local = states.shape[0]
    total = local * cycle_size
    begin = (
        jnp.full((total,), very_low, jnp.float32),
        jnp.zeros((total,), jnp.float32),
        jnp.zeros((total,), jnp.float32),
    )
    token_rows = lax.all_gather(states, TOK, axis=0, tiled=True)
    target_ids = lax.all_gather(targets, TOK, axis=0, tiled=True)
    current = [member for member in begin]
    updated = absorb(current[0], current[1], current[2], token_rows, target_ids, head, first_col)
    highest, scaled, picked = tuple((fresh for fresh in updated))
    highest, scaled, picked = merged_by_axis((highest, scaled, picked), BLK_TOK, combine_stats)
    own_start = lax.axis_index(TOK) * local
    highest = lax.dynamic_slice_in_dim(highest, own_start, local)
    scaled = lax.dynamic_slice_in_dim(scaled, own_start, local)
    picked = lax.dynamic_slice_in_dim(picked, own_start, local)
    excess = highest + jnp.log(scaled) - picked - ref_loss
    seq_count = local * cycle_size // 2
    member = (seq_ids[:, None] == lax.iota(jnp.int32, seq_count)[None, :]).astype(jnp.float32)
    totals = jnp.dot(excess, member, precision=lax.Precision.HIGHEST)
    counts = jnp.sum(member, axis=0)
    totals, counts = packed_total((totals, counts), TOK)
    return (excess, totals / counts)


def solution(mesh):
    torus = Mesh(mesh.devices.reshape(2, 4, 2, 8, 2), ("blk_0", "blk_1", "tok_0", "tok_1", "tok_2"))
    return jax.shard_map(
        on_device,
        mesh=torus,
        in_specs=(P(TOK, None), P(None, BLK_TOK), P(TOK), P(TOK), P(TOK)),
        out_specs=(P(TOK), P()),
        check_vma=False,
    )
```

profile of v0, /device:TPU:1, one launch (start us, length us, event | category | flops | bytes accessed | tf_op | source)
XLA Modules:
  0.0 171.1 jit_solution(2445208449246371563)
XLA Ops:
  7.2 0.0 all-gather.12.cloned.1.call-start
  7.2 0.7 all-gather.12.cloned.1.call-update
  7.9 1.3 dynamic-slice.1
  9.8 0.9 dynamic-update-slice
  10.7 17.2 %all-reduce = s32[1024]{0:T(1024)S(1)} all-reduce(s32[1024]{0:T(1024)S(1)} %dynamic-update-slice), channel_id=1, replica_groups=mesh['blk_0'=2,'blk_1'=4,'tok_0'=2,'tok_1'=8,'tok_2'=2] {'tok_0','tok_1'..., use_global_device_ids=true, to_apply=%add | all-reduce | flops 1024 | bytes 8192
  27.9 0.7 convert_reduce_fusion
  28.7 56.3 %all-gather.12.cloned.1.call-done = bf16[1024,3584]{1,0:T(8,128)(2,1)} async-done(((bf16[32,3584]{1,0:T(8,128)(2,1)}), bf16[1024,3584]{1,0:T(8,128)(2,1)}) %all-gather.12.cloned.1.call-update) | async-done | bytes 7340048 | tf_op jit(solution)/shard_map/all_gather | solution.py:89
  84.9 12.2 %fusion.63 = (f32[1024]{0:T(1024)S(1)}, f32[1024,1024]{0,1:T(8,128)S(1)}) fusion(bf16[1024,3584]{1,0:T(8,128)(2,1)} %all-gather.12.cloned.1.call-done, bf16[3584,1024]{1,0:T(8,128)(2,1)} %param.6), kind=kOutput, calls=%fused_computation.118 | convolution fusion | flops 7517240320 | bytes 18878464 | tf_op jit(solution)/shard_map/dot_general | solution.py:60
  97.2 0.0 copy-start
  97.2 0.0 copy-start.1
  97.2 1.4 exponential_reduce_fusion
  98.7 4.8 %all-gather.5 = f32[2,3,1024]{2,1,0:T(4,128)S(1)} all-gather(f32[1,3,1024]{2,1,0:T(4,128)S(1)} %maximum_bitcast_fusion), channel_id=2, replica_groups=mesh['blk_0'=2,'blk_1'=4,'tok_0'=2,'tok_1'=8,'tok_2'=2] {'blk_0'}, dimensions={0}, use_global_device_ids=true | all-gather | bytes 36864 | tf_op jit(solution)/shard_map/all_gather | solution.py:21
  103.5 9.3 %all-gather.6 = f32[4,3,1024]{2,1,0:T(4,128)S(1)} all-gather(f32[1,3,1024]{2,1,0:T(4,128)S(1)} %maximum_bitcast_fusion.1), channel_id=3, replica_groups=mesh['blk_0'=2,'blk_1'=4,'tok_0'=2,'tok_1'=8,'tok_2'=2] {'blk_1'}, dimensions={0}, use_global_device_ids=true | all-gather | bytes 61440 | tf_op jit(solution)/shard_map/all_gather | solution.py:21
  112.8 0.1 fusion.30
  112.9 3.5 %all-gather.7 = f32[2,3,1024]{2,1,0:T(4,128)S(1)} all-gather(f32[1,3,1024]{2,1,0:T(4,128)S(1)} %maximum_bitcast_fusion.2), channel_id=4, replica_groups=mesh['blk_0'=2,'blk_1'=4,'tok_0'=2,'tok_1'=8,'tok_2'=2] {'tok_0'}, dimensions={0}, use_global_device_ids=true | all-gather | bytes 36864 | tf_op jit(solution)/shard_map/all_gather | solution.py:21
  116.5 18.3 %all-gather.8 = f32[8,3,1024]{2,1,0:T(4,128)S(1)} all-gather(f32[1,3,1024]{2,1,0:T(4,128)S(1)} %maximum_bitcast_fusion.3), channel_id=5, replica_groups=mesh['blk_0'=2,'blk_1'=4,'tok_0'=2,'tok_1'=8,'tok_2'=2] {'tok_1'}, dimensions={0}, use_global_device_ids=true | all-gather | bytes 110592 | tf_op jit(solution)/shard_map/all_gather | solution.py:21
  134.8 0.1 fusion.4
  135.0 13.0 %all-gather.9 = f32[2,3,1024]{2,1,0:T(4,128)S(1)} all-gather(f32[1,3,1024]{2,1,0:T(4,128)S(1)} %maximum_bitcast_fusion.4), channel_id=6, replica_groups=mesh['blk_0'=2,'blk_1'=4,'tok_0'=2,'tok_1'=8,'tok_2'=2] {'tok_2'}, dimensions={0}, use_global_device_ids=true | all-gather | bytes 36864 | tf_op jit(solution)/shard_map/all_gather | solution.py:21
  148.0 0.0 copy-done
  148.0 0.1 fusion.56
  148.1 0.0 copy-done.1
  148.1 0.0 copy-start.2
  148.1 0.2 fusion
  148.3 0.1 broadcast_in_dim.10
  148.4 15.2 %all_to_all.6 = f32[32,1,1024]{2,1,0:T(1,128)S(1)} all-to-all(f32[32,1,1024]{2,1,0:T(1,128)S(1)} %broadcast_in_dim.10), channel_id=1, replica_groups=mesh['blk_0'=2,'blk_1'=4,'tok_0'=2,'tok_1'=8,'tok_2'=2] {'tok_0','tok_1'..., dimensions={0} | all-to-all | bytes 262144 | tf_op jit(solution)/shard_map/all_to_all | solution.py:41
  163.6 0.1 reduce_sum.39
  163.7 0.6 slice_divide_fusion
  164.2 0.0 copy-done.2
  (17 shorter events, 0.3 us)
Async XLA Ops:
  7.2 77.8 %all-gather.12.cloned.1.call-start = ((), (), s32[]{:S(2)}) async-start(), calls=%async_computation.1 | async-start | bytes 7569408 | tf_op jit(solution)/shard_map/all_gather | solution.py:89
  97.2 50.8 %copy-start = (f32[32]{0:T(128)S(1)}, f32[32]{0:T(128)}, u32[]{:S(2)}) copy-start(f32[32]{0:T(128)} %param.8) | copy-start | bytes 388
  97.2 50.9 %copy-start.1 = (s32[32]{0:T(128)S(1)}, s32[32]{0:T(128)}, u32[]{:S(2)}) copy-start(s32[32]{0:T(128)} %param.9) | copy-start | bytes 388
  148.1 16.2 %copy-start.2 = (f32[32]{0:T(128)}, f32[32]{0:T(128)S(1)}, u32[]{:S(2)}) copy-start(f32[32]{0:T(128)S(1)} %fusion.56) | copy-start | bytes 388
Sparse Core Ops, SparseCore 0:
  9.8 75.0 all-gather.11
where the time goes:
time: 171 us
  blocking collectives  81.3 us (48%)
  waiting for transfers between devices  57 us (33%)
  between operations  14.8 us (9%)
  matrix products  12.4 us (7%)
  other arithmetic  3.31 us (2%)
  local copies, waits for them, and re-layouts  2.24 us (1%)
    all_gather x1, waiting for transfers between devices, on_device(): token_rows = lax.all_gather(states, TOK, axis=0, tiled=True)  56.3 us
    all_gather x5, blocking collectives, all_in_one(): both, at, found = (lax.all_gather(jnp.concatenate(lines), axis), 0, {})  48.9 us
    unnamed x1, blocking collectives  17.2 us
    all_to_all x1, blocking collectives, copy_for_each(): lax.all_to_all(jnp.broadcast_to(value[None], (devices, *value.shape)), ax...  15.2 us
    dot_general x1, matrix products, absorb(): logits = jnp.dot(token_rows, head, preferred_element_type=jnp.float32)  12.2 us
  transfers between devices with their start and end apart: 1, of which 1 were waited for; matrix products, arithmetic and copies ran while one was open for 2% of the time, Pallas kernels for 0%

commit v1 on v0

--- a/solution.py
+++ b/solution.py
@@ -8,6 +8,9 @@
 BLK = ("blk_0", "blk_1")
 BLK_TOK = ("blk_0", "blk_1", "tok_0", "tok_1", "tok_2")
 very_low = -1e30
+_view_corner = lambda q_in, which_axis: jnp.concatenate(
+    jax.lax.all_to_all(jnp.stack([q_in] * jax.lax.axis_size(which_axis)), which_axis, 0, 0), axis=0
+)
 
 
 def all_in_one(value, axis):
@@ -86,7 +89,7 @@
         jnp.zeros((total,), jnp.float32),
         jnp.zeros((total,), jnp.float32),
     )
-    token_rows = lax.all_gather(states, TOK, axis=0, tiled=True)
+    token_rows = _view_corner(states, TOK)
     target_ids = lax.all_gather(targets, TOK, axis=0, tiled=True)
     current = [member for member in begin]
     updated = absorb(current[0], current[1], current[2], token_rows, target_ids, head, first_col)

time: 171 us -> 267 us (1.56)
  blocking collectives: 81.3 us -> 233 us
  waiting for transfers between devices: 57 us -> 0.01 us
  between operations: 14.8 us -> 1.48 us
  starting transfers between devices: 0.04 us -> 11.2 us
  local copies, waits for them, and re-layouts: 2.24 us -> 5.74 us
    unnamed x1, blocking collectives: 17.2 us -> 169 us
    all_gather x1 -> x0, waiting for transfers between devices: 56.3 us -> none  [on_device(): token_rows = lax.all_gather(states, TOK, axis=0, tiled=True)]
    all_to_all x0 -> x1, starting transfers between devices: none -> 11.2 us  [jax.lax.all_to_all(jnp.stack([q_in] * jax.lax.axis_size(which_axis)), whi...]
    another operation x0 -> x1, local copies, waits for them, and re-layouts: none -> 4.79 us  [jnp.stack([q_in] * jax.lax.axis_size(which_axis))]
    all_gather x5, blocking collectives: 48.9 us -> 51.9 us  [all_in_one(): both, at, found = (lax.all_gather(jnp.concatenate(lines), axis), 0, {})]
    all_to_all x1, blocking collectives: 15.2 us -> 12.4 us  [copy_for_each(): lax.all_to_all(jnp.broadcast_to(value[None], (devices, *value.shape)), ax...]
  transfers between devices with their start and end apart: 1 -> 1, of which waited for: 1 -> 0; matrix products, arithmetic and copies ran while one was open for 2% -> 0% of each run, Pallas kernels for 0% -> 0%
where the time goes in v1:
time: 267 us
  blocking collectives  233 us (87%)
  matrix products  12.5 us (5%)
  starting transfers between devices  11.2 us (4%)
  local copies, waits for them, and re-layouts  5.74 us (2%)
    unnamed x1, blocking collectives  169 us
    all_gather x5, blocking collectives, all_in_one(): both, at, found = (lax.all_gather(jnp.concatenate(lines), axis), 0, {})  51.9 us
    all_to_all x1, blocking collectives, copy_for_each(): lax.all_to_all(jnp.broadcast_to(value[None], (devices, *value.shape)), ax...  12.4 us
    dot_general x1, matrix products, absorb(): logits = jnp.dot(token_rows, head, preferred_element_type=jnp.float32)  12.3 us
    all_to_all x1, starting transfers between devices, jax.lax.all_to_all(jnp.stack([q_in] * jax.lax.axis_size(which_axis)), whi...  11.2 us
  transfers between devices with their start and end apart: 1, of which 0 were waited for; matrix products, arithmetic and copies ran while one was open for 0% of the time, Pallas kernels for 0%

profile of v1, /device:TPU:1, one launch (start us, length us, event | category | flops | bytes accessed | tf_op | source)
XLA Modules:
  0.0 266.9 jit_solution(15062294571861555254)
XLA Ops:
  0.6 4.8 %stack.2 = bf16[32,32,3584]{2,1,0:T(8,128)(2,1)} broadcast(bf16[32,3584]{1,0:T(8,128)(2,1)} %param.5), dimensions={1,2} | broadcast | bytes 7569408 | tf_op jit(solution)/shard_map/stack | solution.py:12
  5.4 0.0 copy-start.4
  5.4 0.0 copy-start.3
  5.4 0.0 copy-start.1
  5.4 11.2 %all-to-all-start = ((bf16[32,32,3584]{2,1,0:T(8,128)(2,1)}), bf16[32,32,3584]{2,1,0:T(8,128)(2,1)}, u32[]{:S(2)}, u32[]{:S(2)}) async-start(bf16[32,32,3584]{2,1,0:T(8,128)(2,1)} %stack.2), calls=%async_computation | async-start | bytes 14680064 | tf_op jit(solution)/shard_map/all_to_all | solution.py:12
  16.7 0.0 copy-done.4
  16.7 0.6 dynamic-slice.1
  17.9 0.0 copy-done.3
  17.9 0.2 dynamic-update-slice
  18.2 169.0 %all-reduce = s32[1024]{0:T(1024)S(1)} all-reduce(s32[1024]{0:T(1024)S(1)} %dynamic-update-slice), channel_id=1, replica_groups=mesh['blk_0'=2,'blk_1'=4,'tok_0'=2,'tok_1'=8,'tok_2'=2] {'tok_0','tok_1'..., use_global_device_ids=true, to_apply=%add | all-reduce | flops 1024 | bytes 8192
  187.2 0.0 copy-done.1
  187.2 0.1 convert_reduce_fusion
  187.3 0.0 all-to-all-done
  187.3 12.3 %fusion.63 = (f32[1024]{0:T(1024)S(1)}, f32[1024,1024]{0,1:T(8,128)S(1)}) fusion(bf16[1024,3584]{1,0:T(8,128)(2,1)} %bitcast, bf16[3584,1024]{1,0:T(8,128)(2,1)} %param.6), kind=kOutput, calls=%fused_computation.118 | convolution fusion | flops 7517240320 | bytes 18878464 | tf_op jit(solution)/shard_map/dot_general | solution.py:63
  199.6 0.0 copy-start
  199.6 1.4 exponential_reduce_fusion
  201.0 4.8 %all-gather.5 = f32[2,3,1024]{2,1,0:T(4,128)S(1)} all-gather(f32[1,3,1024]{2,1,0:T(4,128)S(1)} %maximum_bitcast_fusion), channel_id=2, replica_groups=mesh['blk_0'=2,'blk_1'=4,'tok_0'=2,'tok_1'=8,'tok_2'=2] {'blk_0'}, dimensions={0}, use_global_device_ids=true | all-gather | bytes 36864 | tf_op jit(solution)/shard_map/all_gather | solution.py:24
  205.8 9.5 %all-gather.6 = f32[4,3,1024]{2,1,0:T(4,128)S(1)} all-gather(f32[1,3,1024]{2,1,0:T(4,128)S(1)} %maximum_bitcast_fusion.1), channel_id=3, replica_groups=mesh['blk_0'=2,'blk_1'=4,'tok_0'=2,'tok_1'=8,'tok_2'=2] {'blk_1'}, dimensions={0}, use_global_device_ids=true | all-gather | bytes 61440 | tf_op jit(solution)/shard_map/all_gather | solution.py:24
  215.4 0.1 fusion.30
  215.4 3.3 %all-gather.7 = f32[2,3,1024]{2,1,0:T(4,128)S(1)} all-gather(f32[1,3,1024]{2,1,0:T(4,128)S(1)} %maximum_bitcast_fusion.2), channel_id=4, replica_groups=mesh['blk_0'=2,'blk_1'=4,'tok_0'=2,'tok_1'=8,'tok_2'=2] {'tok_0'}, dimensions={0}, use_global_device_ids=true | all-gather | bytes 36864 | tf_op jit(solution)/shard_map/all_gather | solution.py:24
  218.8 18.2 %all-gather.8 = f32[8,3,1024]{2,1,0:T(4,128)S(1)} all-gather(f32[1,3,1024]{2,1,0:T(4,128)S(1)} %maximum_bitcast_fusion.3), channel_id=5, replica_groups=mesh['blk_0'=2,'blk_1'=4,'tok_0'=2,'tok_1'=8,'tok_2'=2] {'tok_1'}, dimensions={0}, use_global_device_ids=true | all-gather | bytes 110592 | tf_op jit(solution)/shard_map/all_gather | solution.py:24
  237.0 0.1 fusion.4
  237.2 16.2 %all-gather.9 = f32[2,3,1024]{2,1,0:T(4,128)S(1)} all-gather(f32[1,3,1024]{2,1,0:T(4,128)S(1)} %maximum_bitcast_fusion.4), channel_id=6, replica_groups=mesh['blk_0'=2,'blk_1'=4,'tok_0'=2,'tok_1'=8,'tok_2'=2] {'tok_2'}, dimensions={0}, use_global_device_ids=true | all-gather | bytes 36864 | tf_op jit(solution)/shard_map/all_gather | solution.py:24
  253.4 0.0 copy-done
  253.4 0.1 fusion.56
  253.5 0.0 copy-start.2
  253.5 0.2 fusion
  253.7 0.1 broadcast_in_dim.10
  253.8 12.4 %all_to_all.11 = f32[32,1,1024]{2,1,0:T(1,128)S(1)} all-to-all(f32[32,1,1024]{2,1,0:T(1,128)S(1)} %broadcast_in_dim.10), channel_id=1, replica_groups=mesh['blk_0'=2,'blk_1'=4,'tok_0'=2,'tok_1'=8,'tok_2'=2] {'tok_0','tok_1'..., dimensions={0} | all-to-all | bytes 262144 | tf_op jit(solution)/shard_map/all_to_all | solution.py:44
  266.2 0.1 reduce_sum.39
  266.3 0.6 slice_divide_fusion
  266.9 0.0 copy-done.2
  (17 shorter events, 0.3 us)
Async XLA Ops:
  5.4 11.2 %copy-start.4 = (u32[256]{0:T(256)S(1)}, u32[256]{0:T(256)}, u32[]{:S(2)}) copy-start(u32[256]{0:T(256)} %constant.42) | copy-start | bytes 3076
  5.4 12.5 %copy-start.3 = (s32[32]{0:T(128)S(1)}, s32[32]{0:T(128)}, u32[]{:S(2)}) copy-start(s32[32]{0:T(128)} %param.7) | copy-start | bytes 388
  5.4 181.8 %copy-start.1 = (s32[32]{0:T(128)S(1)}, s32[32]{0:T(128)}, u32[]{:S(2)}) copy-start(s32[32]{0:T(128)} %param.9) | copy-start | bytes 388
  5.4 181.9 %all-to-all-start = ((bf16[32,32,3584]{2,1,0:T(8,128)(2,1)}), bf16[32,32,3584]{2,1,0:T(8,128)(2,1)}, u32[]{:S(2)}, u32[]{:S(2)}) async-start(bf16[32,32,3584]{2,1,0:T(8,128)(2,1)} %stack.2), calls=%async_computation | async-start | bytes 14680064 | tf_op jit(solution)/shard_map/all_to_all | solution.py:12
  199.6 53.8 %copy-start = (f32[32]{0:T(128)S(1)}, f32[32]{0:T(128)}, u32[]{:S(2)}) copy-start(f32[32]{0:T(128)} %param.8) | copy-start | bytes 388
  253.5 13.4 %copy-start.2 = (f32[32]{0:T(128)}, f32[32]{0:T(128)S(1)}, u32[]{:S(2)}) copy-start(f32[32]{0:T(128)S(1)} %fusion.56) | copy-start | bytes 388
